TPU v7x, 64 devices: a 2x2x8 block of a 4x4x8 slice. The times are simulated.
64 devices in a mesh: data: 4 (over x, y), stage: 16 (over z, core).
Axes of the slice: x: 2, y: 2, z: 8, core: 2. Of those that a mesh axis runs over, the one named last changes fastest.
The devices are a block of a 4x4x8 slice.
Arguments:
- micro_in: bfloat16 [128, 128, 384], P('data'), parts along dimension 0
- targets: bfloat16 [128, 128, 384], P('data'), parts along dimension 0
- w_in: bfloat16 [16, 2, 384, 1536], P('stage')
- w_out: bfloat16 [16, 2, 1536, 384], P('stage')
Outputs:
- output 1: float32 [64, 2, 384, 1536], P(('data', 'stage')), parts along dimension 0
- output 2: float32 [64, 2, 1536, 384], P(('data', 'stage')), parts along dimension 0
- output 3: float32 [4], P('data'), parts along dimension 0
There are 4 independent parts. A program takes and returns all parts, laid end to end along the dimension named above; an argument that names none is the same for every part.
All inputs are finite; a program needn't handle non-finite values.
Results may differ from a plain program's by a relative error of at most 0.00438966.
Values are sent between devices in bfloat16 or wider.
A program may use at most 768 MiB of HBM per device.

v0:
```python
import functools
import jax
import jax.numpy as jnp
from jax import lax
from jax.sharding import PartitionSpec as P


def gelu_pair(pre_f32):
    gelu_val, pull_fn = jax.vjp(jax.nn.gelu, pre_f32)
    return gelu_val, pull_fn(jnp.ones_like(pre_f32))[0]


def layer_fwd(h_cur, w_a, w_b):
    pre_act = jnp.dot(h_cur, w_a, preferred_element_type=jnp.float32).astype(jnp.bfloat16)
    act_val = jax.nn.gelu(pre_act.astype(jnp.float32)).astype(jnp.bfloat16)
    branch = jnp.dot(act_val, w_b, preferred_element_type=jnp.float32)
    return (h_cur.astype(jnp.float32) + branch).astype(jnp.bfloat16), pre_act


def layer_bwd(grad_h, h_cur, pre_act, w_a, w_b):
    act_f32, gelu_slope = gelu_pair(pre_act.astype(jnp.float32))
    act_val = act_f32.astype(jnp.bfloat16)
    grad_act = jnp.einsum('bd,fd->bf', grad_h, w_b, preferred_element_type=jnp.float32)
    grad_pre = (gelu_slope * grad_act).astype(jnp.bfloat16)
    back_sum = jnp.einsum('bf,df->bd', grad_pre, w_a, preferred_element_type=jnp.float32)
    grad_in = (grad_h.astype(jnp.float32) + back_sum).astype(jnp.bfloat16)
    grad_wa = jnp.einsum('bd,bf->df', h_cur, grad_pre, preferred_element_type=jnp.float32)
    grad_wb = jnp.einsum('bf,bd->fd', act_val, grad_h, preferred_element_type=jnp.float32)
    return grad_in, grad_wa, grad_wb


def schedule(stage_id, slot_idx, stages, num_micro):
    warm_count = stages - stage_id
    lead_steps = slot_idx - stage_id
    half_lead = lead_steps // 2
    warm_ok = (lead_steps >= 0) & (lead_steps < jnp.minimum(warm_count, num_micro))
    steady_ok = (lead_steps >= 0) & (lead_steps % 2 == 0) & (half_lead >= warm_count) & (half_lead < num_micro)
    fwd_micro = jnp.where(warm_ok, lead_steps, half_lead)
    back_steps = slot_idx - (2 * stages - 1 - stage_id)
    bwd_micro = back_steps // 2
    bwd_ok = (back_steps >= 0) & (back_steps % 2 == 0) & (bwd_micro < num_micro)
    top_micro = num_micro - 1
    return warm_ok | steady_ok, jnp.clip(fwd_micro, 0, top_micro), bwd_ok, jnp.clip(bwd_micro, 0, top_micro)


def keep_state(run_state):
    return run_state


def solution(mesh):
    stages = mesh.shape['stage']
    down_pairs = [(src_idx, src_idx + 1) for src_idx in range(stages - 1)]
    up_pairs = [(src_idx + 1, src_idx) for src_idx in range(stages - 1)]

    def per_device(micro_in, targets, w_in, w_out):
        num_micro, tokens, model_dim = micro_in.shape
        hidden_dim = w_in.shape[-1]
        stage_idx = lax.axis_index('stage')
        is_first = stage_idx == 0
        is_last = stage_idx == stages - 1
        w_first = w_in[0]
        w_second = w_out[0]
        loss_scale = 1.0 / (num_micro * tokens * model_dim)

        def run_fwd(run_state, micro_idx):
            act_hold, grad_hold, saved_h, saved_pre, acc_a, acc_b, loss_acc, send_down, send_up = run_state
            x_now = lax.dynamic_index_in_dim(micro_in, micro_idx, 0, keepdims=False)
            h_first = jnp.where(is_first, x_now, act_hold)
            h_mid, pre_first = layer_fwd(h_first, w_first[0], w_second[0])
            h_out, pre_second = layer_fwd(h_mid, w_first[1], w_second[1])
            ring_idx = micro_idx % stages
            saved_h = lax.dynamic_update_index_in_dim(saved_h, jnp.stack([h_first, h_mid]), ring_idx, 0)
            saved_pre = lax.dynamic_update_index_in_dim(saved_pre, jnp.stack([pre_first, pre_second]), ring_idx, 0)
            tgt_now = lax.dynamic_index_in_dim(targets, micro_idx, 0, keepdims=False)
            residual = h_out.astype(jnp.float32) - tgt_now.astype(jnp.float32)
            loss_acc = loss_acc + jnp.where(is_last, 0.5 * jnp.sum(residual * residual) * loss_scale, 0.0)
            grad_hold = jnp.where(is_last, (residual * loss_scale).astype(jnp.bfloat16), grad_hold)
            return (act_hold, grad_hold, saved_h, saved_pre, acc_a, acc_b, loss_acc, h_out, send_up)

        def run_bwd(run_state, micro_idx):
            act_hold, grad_hold, saved_h, saved_pre, acc_a, acc_b, loss_acc, send_down, send_up = run_state
            ring_idx = micro_idx % stages
            h_pair = lax.dynamic_index_in_dim(saved_h, ring_idx, 0, keepdims=False)
            pre_pair = lax.dynamic_index_in_dim(saved_pre, ring_idx, 0, keepdims=False)
            grad_mid, grad_a_high, grad_b_high = layer_bwd(grad_hold, h_pair[1], pre_pair[1], w_first[1], w_second[1])
            grad_low, grad_a_low, grad_b_low = layer_bwd(grad_mid, h_pair[0], pre_pair[0], w_first[0], w_second[0])
            acc_a = acc_a + jnp.stack([grad_a_low, grad_a_high])
            acc_b = acc_b + jnp.stack([grad_b_low, grad_b_high])
            return (act_hold, grad_hold, saved_h, saved_pre, acc_a, acc_b, loss_acc, send_down, grad_low)

        def slot_body(slot_idx, run_state):
            fwd_ok, fwd_micro, bwd_ok, bwd_micro = schedule(stage_idx, slot_idx, stages, num_micro)
            run_state = lax.cond(fwd_ok, functools.partial(run_fwd, micro_idx=fwd_micro), keep_state, run_state)
            run_state = lax.cond(bwd_ok, functools.partial(run_bwd, micro_idx=bwd_micro), keep_state, run_state)
            act_hold, grad_hold, saved_h, saved_pre, acc_a, acc_b, loss_acc, send_down, send_up = run_state
            recv_act = lax.ppermute(send_down, 'stage', down_pairs)
            recv_grad = lax.ppermute(send_up, 'stage', up_pairs)
            prev_fwd = schedule(stage_idx - 1, slot_idx, stages, num_micro)[0]
            next_bwd = schedule(stage_idx + 1, slot_idx, stages, num_micro)[2]
            act_hold = jnp.where(prev_fwd & (stage_idx > 0), recv_act, act_hold)
            grad_hold = jnp.where(next_bwd & (stage_idx < stages - 1), recv_grad, grad_hold)
            return (act_hold, grad_hold, saved_h, saved_pre, acc_a, acc_b, loss_acc, send_down, send_up)

        block_zero = jnp.zeros((tokens, model_dim), jnp.bfloat16)
        init_state = (block_zero, block_zero, jnp.zeros((stages, 2, tokens, model_dim), jnp.bfloat16), jnp.zeros((stages, 2, tokens, hidden_dim), jnp.bfloat16), jnp.zeros((2, model_dim, hidden_dim), jnp.float32), jnp.zeros((2, hidden_dim, model_dim), jnp.float32), jnp.zeros((), jnp.float32), block_zero, block_zero)
        slot_count = 2 * num_micro + 2 * stages - 2
        final_state = lax.fori_loop(0, slot_count, slot_body, init_state)
        loss_total = lax.psum(final_state[6], 'stage')
        return final_state[4][None], final_state[5][None], loss_total.reshape(1)

    return jax.shard_map(per_device, mesh=mesh, in_specs=(P('data'), P('data'), P('stage'), P('stage')), out_specs=(P(('data', 'stage')), P(('data', 'stage')), P('data')), check_vma=False)
```

profile of v0, /device:TPU:21, one launch (start us, length us, event | category | flops | bytes accessed | tf_op | source)
XLA Modules:
  0.0 2595.8 jit_solution(5761641608840903592)
XLA Ops:
  15.3 2556.1 %while.33 = (s32[]{:T(128)}, bf16[128,384]{1,0:T(8,128)(2,1)}, bf16[128,384]{1,0:T(8,128)(2,1)S(1)}, bf16[16,2,128,384]{3,2,1,0:T(8,128)(2,1)}, bf16[16,2,128,15...) while((s32[]{:T(128)}, bf16[128,384]{1,0:T(8,128)(2,1)}, ...), condition=%wide.region_6.7_spmd.clone, body=%wide.region_0.6_spmd.clone.sunk | while | flops 1836122112 | bytes 143722736 | solution.py:107
  396.9 19.2 collective-permute-start
  419.0 38.6 %collective-permute-done.1 = bf16[128,384]{1,0:T(8,128)(2,1)S(1)} collective-permute-done((bf16[128,384]{1,0:T(8,128)(2,1)}, bf16[128,384]{1,0:T(8,128)(2,1)S(1)}, u32[]{:S(2)}, u32[]{:S(2)}) %collective-permute-start.1) | collective-permute-done | bytes 98336 | tf_op jit(solution)/shard_map/while/body/eval_jaxpr/ppermute | solution.py:97
  458.7 20.7 collective-permute-start
  482.2 37.1 %collective-permute-done.1 = bf16[128,384]{1,0:T(8,128)(2,1)S(1)} collective-permute-done((bf16[128,384]{1,0:T(8,128)(2,1)}, bf16[128,384]{1,0:T(8,128)(2,1)S(1)}, u32[]{:S(2)}, u32[]{:S(2)}) %collective-permute-start.1) | collective-permute-done | bytes 98336 | tf_op jit(solution)/shard_map/while/body/eval_jaxpr/ppermute | solution.py:97
  520.4 22.3 collective-permute-start
  545.5 35.7 %collective-permute-done.1 = bf16[128,384]{1,0:T(8,128)(2,1)S(1)} collective-permute-done((bf16[128,384]{1,0:T(8,128)(2,1)}, bf16[128,384]{1,0:T(8,128)(2,1)S(1)}, u32[]{:S(2)}, u32[]{:S(2)}) %collective-permute-start.1) | collective-permute-done | bytes 98336 | tf_op jit(solution)/shard_map/while/body/eval_jaxpr/ppermute | solution.py:97
  582.2 23.8 collective-permute-start
  608.8 35.3 %collective-permute-done.1 = bf16[128,384]{1,0:T(8,128)(2,1)S(1)} collective-permute-done((bf16[128,384]{1,0:T(8,128)(2,1)}, bf16[128,384]{1,0:T(8,128)(2,1)S(1)}, u32[]{:S(2)}, u32[]{:S(2)}) %collective-permute-start.1) | collective-permute-done | bytes 98336 | tf_op jit(solution)/shard_map/while/body/eval_jaxpr/ppermute | solution.py:97
  645.1 25.3 collective-permute-start
  673.3 32.7 %collective-permute-done.1 = bf16[128,384]{1,0:T(8,128)(2,1)S(1)} collective-permute-done((bf16[128,384]{1,0:T(8,128)(2,1)}, bf16[128,384]{1,0:T(8,128)(2,1)S(1)}, u32[]{:S(2)}, u32[]{:S(2)}) %collective-permute-start.1) | collective-permute-done | bytes 98336 | tf_op jit(solution)/shard_map/while/body/eval_jaxpr/ppermute | solution.py:97
  707.0 26.7 %collective-permute-start = (bf16[128,384]{1,0:T(8,128)(2,1)}, bf16[128,384]{1,0:T(8,128)(2,1)S(1)}, u32[]{:S(2)}, u32[]{:S(2)}) collective-permute-start(bf16[128,384]{1,0:T(8,128)(2,1)} %get-tuple-element.1072), channel_id=1, source_target_pairs={{0,1},{1,2},{2,3},{3,4},{4,5},{5,6},{6,7},{7,8},{8,9},{9,10},{10,1... | collective-permute-start | bytes 294920 | tf_op jit(solution)/shard_map/while/body/eval_jaxpr/ppermute | solution.py:96
  736.6 31.1 %collective-permute-done.1 = bf16[128,384]{1,0:T(8,128)(2,1)S(1)} collective-permute-done((bf16[128,384]{1,0:T(8,128)(2,1)}, bf16[128,384]{1,0:T(8,128)(2,1)S(1)}, u32[]{:S(2)}, u32[]{:S(2)}) %collective-permute-start.1) | collective-permute-done | bytes 98336 | tf_op jit(solution)/shard_map/while/body/eval_jaxpr/ppermute | solution.py:97
  780.2 16.9 conditional.7
  815.7 19.3 collective-permute-start.1
  840.8 16.9 conditional.7
  876.2 19.3 collective-permute-start.1
  901.4 16.9 conditional.7
  936.9 19.3 collective-permute-start.1
  962.0 16.9 conditional.7
  997.5 19.3 collective-permute-start.1
  1022.6 16.9 conditional.7
  1058.0 19.3 collective-permute-start.1
  1083.1 16.9 conditional.7
  1118.6 19.3 collective-permute-start.1
  1143.7 16.9 conditional.7
  1179.2 19.3 collective-permute-start.1
  1204.3 16.9 conditional.7
  1239.8 19.3 collective-permute-start.1
  1264.9 16.9 conditional.7
  1300.4 19.3 collective-permute-start.1
  1325.5 16.9 conditional.7
  1361.0 19.3 collective-permute-start.1
  1386.1 16.9 conditional.7
  1421.5 19.3 collective-permute-start.1
  1446.6 16.9 conditional.7
  1482.2 19.3 collective-permute-start.1
  1507.3 16.9 conditional.7
  1542.8 19.3 collective-permute-start.1
  1567.9 16.9 conditional.7
  1603.4 19.3 collective-permute-start.1
  1628.5 16.9 conditional.7
  1664.0 19.3 collective-permute-start.1
  1689.1 16.9 conditional.7
  1724.5 19.3 collective-permute-start.1
  1749.7 16.9 conditional.7
  1785.1 19.3 collective-permute-start.1
  1810.2 16.9 conditional.7
  1836.1 19.3 collective-permute-start.1
  1887.2 19.3 collective-permute-start.1
  1938.2 19.3 collective-permute-start.1
  1989.3 19.3 collective-permute-start.1
  2040.3 19.3 collective-permute-start.1
  2091.4 19.3 collective-permute-start.1
  2142.4 19.3 collective-permute-start.1
  2193.5 19.3 collective-permute-start.1
  2244.6 19.3 collective-permute-start.1
  2295.7 19.3 collective-permute-start.1
  2346.8 19.3 collective-permute-start.1
  2397.8 19.3 collective-permute-start.1
  2449.0 19.3 collective-permute-start.1
  2500.0 19.3 collective-permute-start.1
  2551.2 19.3 collective-permute-start.1
  2571.4 24.5 psum.7
  (1946 shorter events, 2096.4 us)
Async XLA Ops:
  416.3 41.4 %collective-permute-start.1 = (bf16[128,384]{1,0:T(8,128)(2,1)}, bf16[128,384]{1,0:T(8,128)(2,1)S(1)}, u32[]{:S(2)}, u32[]{:S(2)}) collective-permute-start(bf16[128,384]{1,0:T(8,128)(2,1)} %get-tuple-element.1073), channel_id=1, source_target_pairs={{1,0},{2,1},{3,2},{4,3},{5,4},{6,5},{7,6},{8,7},{9,8},{10,9},{11,1... | collective-permute-start | bytes 294920 | tf_op jit(solution)/shard_map/while/body/eval_jaxpr/ppermute | solution.py:97
  458.7 22.9 collective-permute-start
  479.5 39.9 %collective-permute-start.1 = (bf16[128,384]{1,0:T(8,128)(2,1)}, bf16[128,384]{1,0:T(8,128)(2,1)S(1)}, u32[]{:S(2)}, u32[]{:S(2)}) collective-permute-start(bf16[128,384]{1,0:T(8,128)(2,1)} %get-tuple-element.1073), channel_id=1, source_target_pairs={{1,0},{2,1},{3,2},{4,3},{5,4},{6,5},{7,6},{8,7},{9,8},{10,9},{11,1... | collective-permute-start | bytes 294920 | tf_op jit(solution)/shard_map/while/body/eval_jaxpr/ppermute | solution.py:97
  520.4 24.4 collective-permute-start
  542.7 38.4 %collective-permute-start.1 = (bf16[128,384]{1,0:T(8,128)(2,1)}, bf16[128,384]{1,0:T(8,128)(2,1)S(1)}, u32[]{:S(2)}, u32[]{:S(2)}) collective-permute-start(bf16[128,384]{1,0:T(8,128)(2,1)} %get-tuple-element.1073), channel_id=1, source_target_pairs={{1,0},{2,1},{3,2},{4,3},{5,4},{6,5},{7,6},{8,7},{9,8},{10,9},{11,1... | collective-permute-start | bytes 294920 | tf_op jit(solution)/shard_map/while/body/eval_jaxpr/ppermute | solution.py:97
  582.2 25.9 collective-permute-start
  606.0 38.1 %collective-permute-start.1 = (bf16[128,384]{1,0:T(8,128)(2,1)}, bf16[128,384]{1,0:T(8,128)(2,1)S(1)}, u32[]{:S(2)}, u32[]{:S(2)}) collective-permute-start(bf16[128,384]{1,0:T(8,128)(2,1)} %get-tuple-element.1073), channel_id=1, source_target_pairs={{1,0},{2,1},{3,2},{4,3},{5,4},{6,5},{7,6},{8,7},{9,8},{10,9},{11,1... | collective-permute-start | bytes 294920 | tf_op jit(solution)/shard_map/while/body/eval_jaxpr/ppermute | solution.py:97
  645.1 27.5 %collective-permute-start = (bf16[128,384]{1,0:T(8,128)(2,1)}, bf16[128,384]{1,0:T(8,128)(2,1)S(1)}, u32[]{:S(2)}, u32[]{:S(2)}) collective-permute-start(bf16[128,384]{1,0:T(8,128)(2,1)} %get-tuple-element.1072), channel_id=1, source_target_pairs={{0,1},{1,2},{2,3},{3,4},{4,5},{5,6},{6,7},{7,8},{8,9},{9,10},{10,1... | collective-permute-start | bytes 294920 | tf_op jit(solution)/shard_map/while/body/eval_jaxpr/ppermute | solution.py:96
  670.6 35.4 %collective-permute-start.1 = (bf16[128,384]{1,0:T(8,128)(2,1)}, bf16[128,384]{1,0:T(8,128)(2,1)S(1)}, u32[]{:S(2)}, u32[]{:S(2)}) collective-permute-start(bf16[128,384]{1,0:T(8,128)(2,1)} %get-tuple-element.1073), channel_id=1, source_target_pairs={{1,0},{2,1},{3,2},{4,3},{5,4},{6,5},{7,6},{8,7},{9,8},{10,9},{11,1... | collective-permute-start | bytes 294920 | tf_op jit(solution)/shard_map/while/body/eval_jaxpr/ppermute | solution.py:97
  707.0 28.9 %collective-permute-start = (bf16[128,384]{1,0:T(8,128)(2,1)}, bf16[128,384]{1,0:T(8,128)(2,1)S(1)}, u32[]{:S(2)}, u32[]{:S(2)}) collective-permute-start(bf16[128,384]{1,0:T(8,128)(2,1)} %get-tuple-element.1072), channel_id=1, source_target_pairs={{0,1},{1,2},{2,3},{3,4},{4,5},{5,6},{6,7},{7,8},{8,9},{9,10},{10,1... | collective-permute-start | bytes 294920 | tf_op jit(solution)/shard_map/while/body/eval_jaxpr/ppermute | solution.py:96
  733.8 33.9 %collective-permute-start.1 = (bf16[128,384]{1,0:T(8,128)(2,1)}, bf16[128,384]{1,0:T(8,128)(2,1)S(1)}, u32[]{:S(2)}, u32[]{:S(2)}) collective-permute-start(bf16[128,384]{1,0:T(8,128)(2,1)} %get-tuple-element.1073), channel_id=1, source_target_pairs={{1,0},{2,1},{3,2},{4,3},{5,4},{6,5},{7,6},{8,7},{9,8},{10,9},{11,1... | collective-permute-start | bytes 294920 | tf_op jit(solution)/shard_map/while/body/eval_jaxpr/ppermute | solution.py:97
  768.7 30.4 %collective-permute-start = (bf16[128,384]{1,0:T(8,128)(2,1)}, bf16[128,384]{1,0:T(8,128)(2,1)S(1)}, u32[]{:S(2)}, u32[]{:S(2)}) collective-permute-start(bf16[128,384]{1,0:T(8,128)(2,1)} %get-tuple-element.1072), channel_id=1, source_target_pairs={{0,1},{1,2},{2,3},{3,4},{4,5},{5,6},{6,7},{7,8},{8,9},{9,10},{10,1... | collective-permute-start | bytes 294920 | tf_op jit(solution)/shard_map/while/body/eval_jaxpr/ppermute | solution.py:96
  813.6 21.4 collective-permute-start
  836.9 22.8 collective-permute-start
  897.5 22.8 collective-permute-start
  958.1 22.8 collective-permute-start
  1018.7 22.8 collective-permute-start
  1056.0 21.4 collective-permute-start
  1079.3 22.8 collective-permute-start
  1116.6 21.4 collective-permute-start
  1139.8 22.8 collective-permute-start
  1200.4 22.8 collective-permute-start
  1237.8 21.4 collective-permute-start
  1261.0 22.8 collective-permute-start
  1321.6 22.8 collective-permute-start
  1382.2 22.8 collective-permute-start
  1442.8 22.8 collective-permute-start
  1503.4 22.8 collective-permute-start
  1564.0 22.8 collective-permute-start
  1624.6 22.8 collective-permute-start
  1662.0 21.4 collective-permute-start
  1685.2 22.8 collective-permute-start
  1722.5 21.4 collective-permute-start
  1745.8 22.8 collective-permute-start
  1806.3 22.8 collective-permute-start
  1834.1 21.4 collective-permute-start
  1836.1 22.2 collective-permute-start.1
  1885.2 21.4 collective-permute-start
  1887.2 22.1 collective-permute-start.1
  1936.2 21.4 collective-permute-start
  1938.2 22.2 collective-permute-start.1
  1987.3 21.4 collective-permute-start
  1989.3 22.1 collective-permute-start.1
  2038.2 21.4 collective-permute-start
  2040.3 22.2 collective-permute-start.1
  2089.3 21.4 collective-permute-start
  2091.4 22.1 collective-permute-start.1
  2140.3 21.4 collective-permute-start
  2142.4 22.2 collective-permute-start.1
  2191.4 21.4 collective-permute-start
  2193.5 22.2 collective-permute-start.1
  2242.5 21.4 collective-permute-start
  2244.6 22.2 collective-permute-start.1
  2293.6 21.4 collective-permute-start
  2295.7 22.2 collective-permute-start.1
  2344.7 21.4 collective-permute-start
  2346.8 22.2 collective-permute-start.1
  2395.8 21.4 collective-permute-start
  2397.8 22.2 collective-permute-start.1
  2446.9 21.4 collective-permute-start
  2449.0 22.2 collective-permute-start.1
  2498.0 21.4 collective-permute-start
  2500.0 22.2 collective-permute-start.1
  2549.1 21.4 collective-permute-start
  (381 other events, 2462.9 us)
where the time goes:
time: 2610 us; the launch traced here: 2600 us
  starting transfers between devices  1110 us (43%)
  matrix products  538 us (21%)
  waiting for transfers between devices  420 us (16%)
  other arithmetic  359 us (14%)
  local copies, waits for them, and re-layouts  85.8 us (3%)
  loops' own time  55.6 us (2%)
    ppermute x94, starting transfers between devices, slot_body(): recv_grad = lax.ppermute(send_up, 'stage', up_pairs)  758 us
    ppermute x94, waiting for transfers between devices, slot_body(): recv_grad = lax.ppermute(send_up, 'stage', up_pairs)  420 us
    ppermute x94, starting transfers between devices, slot_body(): recv_act = lax.ppermute(send_down, 'stage', down_pairs)  354 us
    dot_general x64, matrix products, layer_bwd(): jnp.einsum('bd,fd->bf', grad_h, w_b, preferred_element_type=jnp.float32)  132 us
    dot_general x64, matrix products, layer_fwd(): branch = jnp.dot(act_val, w_b, preferred_element_type=jnp.float32)  125 us
    dot_general x64, matrix products, layer_bwd(): jnp.einsum('bf,bd->fd', act_val, grad_h, preferred_element_type=jnp.float32)  111 us
    dot_general x64, matrix products, layer_bwd(): jnp.einsum('bd,bf->df', h_cur, grad_pre, preferred_element_type=jnp.float32)  93.1 us
    while x94, other arithmetic  85.8 us
  transfers between devices with their start and end apart: 188, of which 94 were waited for; matrix products, arithmetic and copies ran while one was open for 20% of the time, Pallas kernels for 0%

commit v1 on v0

v1 whole, which is shorter than its diff:
```python
import functools

import jax
import jax.numpy as jnp
import numpy as np
from jax import lax
from jax.experimental import pallas as pl
from jax.experimental.pallas import tpu as pltpu
from jax.sharding import PartitionSpec as P

BF16 = jnp.bfloat16
F32 = jnp.float32
C0 = float(np.sqrt(2.0 / np.pi))
C1 = C0 * 0.044715
TILE = 256
LAG = 2


def dot(x, w):
    return jnp.dot(x, w, preferred_element_type=F32)


def gelu(u):
    t = jnp.tanh(u * (C0 + C1 * (u * u)))
    return u * (0.5 * t + 0.5)


def gelu_slope(u_bf):
    u = jnp.clip(u_bf, -1024.0, 1024.0).astype(F32)
    u2 = u * u
    t = jnp.tanh(u * (C0 + C1 * u2))
    w = u * (0.5 * C0 + (1.5 * C1) * u2)
    return (1.0 + t) * (0.5 + (1.0 - t) * w)


def layer(x, w1, w2, tiles, middle):
    acc = None
    mids = []
    for n in range(tiles + LAG):
        if n < tiles:
            mids.append(middle(n, dot(x, w1[:, n * TILE:(n + 1) * TILE])))
        if n >= LAG:
            k = n - LAG
            part = dot(mids[k], w2[k * TILE:(k + 1) * TILE, :])
            acc = part if acc is None else acc + part
    return (x.astype(F32) + acc).astype(BF16)


def pipeline_kernel(stages, x_hbm, t_hbm, wi_hbm, wo_hbm, sh, sa, se, sg, loss_ref, wa, wb, wat, wbt, hin, gin, us, ast, hst,
                    est, gst, hsend, gsend, lacc, lpeer, lrecv, wa_sem, wb_sem, wsend_sem, fin_sem, gin_sem, hs_sem, gs_sem,
                    fa_sem, fh_sem, be_sem, bg_sem, stash_sem, lp_sem, lr_sem):
    k = lax.axis_index('stage')
    chips = stages // 2
    s = k // 2
    c = k % 2
    last = chips - 1
    peer = k + 1 - 2 * c
    num_micro, tokens, dim = x_hbm.shape
    hidden = wi_hbm.shape[-1]
    own = wi_hbm.shape[0]
    layers = 2 * own
    nb = num_micro // 2
    tiles = hidden // TILE
    scale = 1.0 / (num_micro * tokens * dim)

    def dev(idx):
        return {'stage': idx}

    def copy(src, dst, sem):
        return pltpu.make_async_copy(src, dst, sem)

    def remote(src, dst, send, recv, idx):
        return pltpu.make_async_remote_copy(src_ref=src, dst_ref=dst, send_sem=send, recv_sem=recv, device_id=dev(idx),
                                            device_id_type=pl.DeviceIdType.MESH)

    for ll in range(own):
        copy(wi_hbm.at[ll], wa.at[own * c + ll], wa_sem.at[own * c + ll]).start()
        copy(wo_hbm.at[ll], wb.at[own * c + ll], wb_sem.at[own * c + ll]).start()

    @pl.when(s == 0)
    def _():
        @pl.loop(0, nb)
        def _(i):
            copy(x_hbm.at[c * nb + i], hin.at[i], fin_sem.at[i]).start()

    @pl.when(s == last)
    def _():
        @pl.loop(0, nb)
        def _(i):
            copy(t_hbm.at[c * nb + i], gin.at[i], gin_sem.at[i]).start()

    barrier = pltpu.get_barrier_semaphore()
    pl.semaphore_signal(barrier, inc=1, device_id=dev(peer), device_id_type=pl.DeviceIdType.MESH)

    @pl.when(s > 0)
    def _():
        pl.semaphore_signal(barrier, inc=1, device_id=dev(k - 2), device_id_type=pl.DeviceIdType.MESH)

    @pl.when(s < last)
    def _():
        pl.semaphore_signal(barrier, inc=1, device_id=dev(k + 2), device_id_type=pl.DeviceIdType.MESH)

    pl.semaphore_wait(barrier, 1 + jnp.where(s > 0, 1, 0) + jnp.where(s < last, 1, 0))

    def weight_sends():
        out = []
        for ll in range(own):
            l = own * c + ll
            out.append(remote(wi_hbm.at[ll], wa.at[l], wsend_sem.at[2 * ll], wa_sem.at[l], peer))
            out.append(remote(wo_hbm.at[ll], wb.at[l], wsend_sem.at[2 * ll + 1], wb_sem.at[l], peer))
        return out

    for send in weight_sends():
        send.start()
    lacc[...] = jnp.zeros_like(lacc)
    for l in range(layers):
        copy(wa.at[l], wa.at[l], wa_sem.at[l]).wait()
        copy(wb.at[l], wb.at[l], wb_sem.at[l]).wait()

    def transposes():
        @pl.loop(0, layers * tiles)
        def _(j):
            l = j // tiles
            at = pl.ds(pl.multiple_of((j % tiles) * TILE, TILE), TILE)
            wat[l, at, :] = wa[l, :, at].T
            wbt[l, :, at] = wb[l, at, :].T

    warm = jnp.minimum(nb, 1 + (13 * (last - s) + 4) // 5)

    @pl.when(s > 0)
    def _():
        transposes()

    def stash_forward(i, par):
        for l in range(layers):
            ll = l % own
            a_at, h_at = ast.at[par, l], (hin.at[i] if l == 0 else hst.at[par, l - 1])
            yield l // own, (a_at, sa.at[ll, c, i], fa_sem.at[par, l], stash_sem.at[1, ll]), (h_at, sh.at[ll, c, i], fh_sem.at[par, l], stash_sem.at[0, ll])

    def stash_backward(i, par):
        for l in range(layers):
            ll = l % own
            e_at, g_at = est.at[par, l], (gin.at[i] if l == layers - 1 else gst.at[par, l])
            yield l // own, (e_at, se.at[ll, c, i], be_sem.at[par, l], stash_sem.at[2, ll]), (g_at, sg.at[ll, c, i], bg_sem.at[par, l], stash_sem.at[3, ll])

    def stash_start(pairs):
        for owner, one, two in pairs:
            @pl.when(c == owner)
            def _():
                copy(*one[:3]).start()
                copy(*two[:3]).start()

            @pl.when(c != owner)
            def _():
                remote(*one, peer).start()
                remote(*two, peer).start()

    def stash_wait(pairs):
        for owner, one, two in pairs:
            @pl.when(c == owner)
            def _():
                copy(*one[:3]).wait()
                copy(*two[:3]).wait()

            @pl.when(c != owner)
            def _():
                remote(*one, peer).wait_send()
                remote(*two, peer).wait_send()

    def h_send(i, par):
        return remote(hsend.at[par], hin.at[i], hs_sem.at[par], fin_sem.at[i], k + 2)

    def g_send(i, par):
        return remote(gsend.at[par], gin.at[i], gs_sem.at[par], gin_sem.at[i], k - 2)

    def forward(i):
        par = i % 2

        @pl.when(i >= 2)
        def _():
            stash_wait(stash_forward(i - 2, par))

            @pl.when(s < last)
            def _():
                h_send(i - 2, par).wait_send()

        copy(hin.at[i], hin.at[i], fin_sem.at[i]).wait()
        x = hin[i]
        for l in range(layers):
            if l > 0:
                hst[par, l - 1] = x

            def middle(n, p, l=l):
                at = slice(n * TILE, (n + 1) * TILE)
                u = p.astype(BF16)
                us[i, l, :, at] = u
                a = gelu(u.astype(F32)).astype(BF16)
                ast[par, l, :, at] = a
                return a

            x = layer(x, wa.at[l], wb.at[l], tiles, middle)
        hsend[par] = x

        @pl.when(s < last)
        def _():
            h_send(i, par).start()

        stash_start(stash_forward(i, par))

        @pl.when(s == last)
        def _():
            copy(gin.at[i], gin.at[i], gin_sem.at[i]).wait()
            r = hsend[par].astype(F32) - gin[i].astype(F32)
            gin[i] = (r * scale).astype(BF16)
            lacc[...] += jnp.sum((r * r).reshape(tokens // 8, 8, dim), axis=0)

            @pl.when(i == nb - 1)
            def _():
                remote(lacc, lpeer, lp_sem.at[0], lp_sem.at[1], peer).start()

    def backward(i):
        par = i % 2

        @pl.when(i >= 2)
        def _():
            stash_wait(stash_backward(i - 2, par))

            @pl.when(s > 0)
            def _():
                g_send(i - 2, par).wait_send()

        @pl.when(s < last)
        def _():
            copy(gin.at[i], gin.at[i], gin_sem.at[i]).wait()

        g = gin[i]
        for l in reversed(range(layers)):
            if l < layers - 1:
                gst[par, l] = g

            def middle(n, p, l=l):
                at = slice(n * TILE, (n + 1) * TILE)
                e = (gelu_slope(us[i, l, :, at]) * p).astype(BF16)
                est[par, l, :, at] = e
                return e

            g = layer(g, wbt.at[l], wat.at[l], tiles, middle)
        gsend[par] = g

        @pl.when(s > 0)
        def _():
            g_send(i, par).start()

        stash_start(stash_backward(i, par))

        @pl.when(i == nb - 1)
        def _():
            @pl.when(s == last)
            def _():
                remote(lacc, lpeer, lp_sem.at[0], lp_sem.at[1], peer).wait()
                lrecv[...] = jnp.full(lrecv.shape, jnp.sum(lacc[...] + lpeer[...]) * (0.5 * scale), F32)

            @pl.when(s < last)
            def _():
                copy(lrecv, lrecv, lr_sem.at[1]).wait()

            loss_ref[...] = lrecv[...]

            @pl.when(s > 0)
            def _():
                send = remote(lrecv, lrecv, lr_sem.at[0], lr_sem.at[1], k - 2)
                send.start()
                send.wait_send()

    @pl.loop(0, nb + warm)
    def _(j):
        @pl.when((j == warm) & (s == 0))
        def _():
            transposes()

        @pl.when(j >= warm)
        def _():
            backward(j - warm)

        @pl.when(j < nb)
        def _():
            forward(j)

    for send in weight_sends():
        send.wait_send()
    for i in (nb - 2, nb - 1):
        stash_wait(stash_forward(i, i % 2))
        stash_wait(stash_backward(i, i % 2))

        @pl.when(s < last)
        def _():
            h_send(i, i % 2).wait_send()

        @pl.when(s > 0)
        def _():
            g_send(i, i % 2).wait_send()

    for ll in range(own):
        for kind, ref in enumerate((sh, sa, se, sg)):
            there = ref.at[ll, 1 - c]
            copy(there, there, stash_sem.at[kind, ll]).wait()


def solution(mesh):
    stages = mesh.shape['stage']

    def per_device(micro_in, targets, w_in, w_out):
        num_micro, tokens, dim = micro_in.shape
        own, hidden = w_in.shape[1], w_in.shape[3]
        layers = 2 * own
        nb = num_micro // 2
        hbm = pl.BlockSpec(memory_space=pl.ANY)
        vm = pltpu.VMEM
        dma = pltpu.SemaphoreType.DMA
        wide = jax.ShapeDtypeStruct((own, 2, nb, tokens, hidden), BF16)
        narrow = jax.ShapeDtypeStruct((own, 2, nb, tokens, dim), BF16)
        sh, sa, se, sg, loss = pl.pallas_call(
            functools.partial(pipeline_kernel, stages),
            out_shape=(narrow, wide, wide, narrow, jax.ShapeDtypeStruct((8, 128), F32)),
            in_specs=[hbm] * 4,
            out_specs=(hbm, hbm, hbm, hbm, pl.BlockSpec(memory_space=pltpu.VMEM)),
            scratch_shapes=[
                vm((layers, dim, hidden), BF16), vm((layers, hidden, dim), BF16),
                vm((layers, hidden, dim), BF16), vm((layers, dim, hidden), BF16),
                vm((nb, tokens, dim), BF16), vm((nb, tokens, dim), BF16),
                vm((nb, layers, tokens, hidden), BF16),
                vm((2, layers, tokens, hidden), BF16), vm((2, layers - 1, tokens, dim), BF16),
                vm((2, layers, tokens, hidden), BF16), vm((2, layers - 1, tokens, dim), BF16),
                vm((2, tokens, dim), BF16), vm((2, tokens, dim), BF16),
                vm((8, dim), F32), vm((8, dim), F32), vm((8, 128), F32),
                dma((layers,)), dma((layers,)), dma((2 * own,)), dma((nb,)), dma((nb,)), dma((2,)), dma((2,)),
                dma((2, layers)), dma((2, layers)), dma((2, layers)), dma((2, layers)), dma((4, own)), dma((2,)), dma((2,)),
            ],
            compiler_params=pltpu.CompilerParams(collective_id=0, has_side_effects=True, vmem_limit_bytes=67043328),
            name='pipeline',
        )(micro_in, targets, w_in[0], w_out[0])

        def grad(left, right):
            left = left.reshape(own, num_micro * tokens, left.shape[-1])
            right = right.reshape(own, num_micro * tokens, right.shape[-1])
            return jnp.einsum('lti,ltj->lij', left, right, preferred_element_type=F32)

        return grad(sh, se)[None], grad(sa, sg)[None], loss[0, :1]

    return jax.shard_map(per_device, mesh=mesh, in_specs=(P('data'), P('data'), P('stage'), P('stage')),
                         out_specs=(P(('data', 'stage')), P(('data', 'stage')), P('data')), check_vma=False)
```

time: 2610 us -> 248 us (0.10)
  starting transfers between devices: 1110 us -> 0 us
  matrix products: 538 us -> 38.4 us
  waiting for transfers between devices: 420 us -> 0 us
  other arithmetic: 359 us -> 0 us
  Pallas kernels: 0 us -> 208 us
  local copies, waits for them, and re-layouts: 85.8 us -> 1.19 us
  loops' own time: 55.6 us -> 0 us
    ppermute x188 -> x0, starting transfers between devices: 1110 us -> none  [the longest x94 758 us: slot_body(): recv_grad = lax.ppermute(send_up, 'stage', up_pairs)]
    dot_general x384 -> x2, matrix products: 538 us -> 38.4 us  [grad(): return jnp.einsum('lti,ltj->lij', left, right, preferred_element_type=F32)]
    ppermute x188 -> x0, waiting for transfers between devices: 420 us -> none  [the longest x94 420 us: slot_body(): recv_grad = lax.ppermute(send_up, 'stage', up_pairs)]
    pallas_call x0 -> x1, Pallas kernels: none -> 208 us  [per_device(): pl.pallas_call(functools.partial(pipeline_kernel, stages), out_shape=(nar...]
    select_n x220 -> x0, other arithmetic: 93.6 us -> none  [the longest x94 62.9 us: slot_body(): act_hold = jnp.where(prev_fwd & (stage_idx > 0), recv_act, act_hold)]
    while x94 -> x0, other arithmetic: 85.8 us -> none
    add x64 -> x0, other arithmetic: 73.1 us -> none  [the longest x32 40.6 us: run_bwd(): acc_a = acc_a + jnp.stack([grad_a_low, grad_a_high])]
    cond x512 -> x0, local copies, waits for them, and re-layouts: 71.2 us -> none
  transfers between devices with their start and end apart: 188 -> 0, of which waited for: 94 -> 0; matrix products, arithmetic and copies ran while one was open for 20% -> 0% of each run, Pallas kernels for 0% -> 0%
where the time goes in v1:
time: 248 us
  Pallas kernels  208 us (84%)
  matrix products  38.4 us (15%)
    pallas_call x1, Pallas kernels, per_device(): pl.pallas_call(functools.partial(pipeline_kernel, stages), out_shape=(nar...  208 us
    dot_general x2, matrix products, grad(): return jnp.einsum('lti,ltj->lij', left, right, preferred_element_type=F32)  38.4 us

profile of v1, /device:TPU:21, one launch (start us, length us, event | category | flops | bytes accessed | tf_op | source)
XLA Modules:
  0.0 247.7 jit_solution(9591440252734429957)
XLA Ops:
  0.6 207.5 %pipeline.1 = (bf16[2,2,16,128,384]{4,3,2,1,0:T(8,128)(2,1)}, bf16[2,2,16,128,1536]{4,3,2,1,0:T(8,128)(2,1)}, bf16[2,2,16,128,1536]{4,3,2,1,0:T(8,128)(2,1)}, bf...) custom-call(bf16[32,128,384]{2,1,0:T(8,128)(2,1)} %x_hbm.1, bf16[32,128,384]{2,1,0:T(8,128)(2,1)} %t_hbm.1, ...), custom_call_target="tpu_custom_call" | custom-call | tf_op jit(solution)/shard_map/pipeline/pallas_call | solution.py:322
  208.2 1.2 slice.3
  209.4 18.2 %convolution_bitcast_fusion = f32[1,2,384,1536]{3,2,1,0:T(8,128)} fusion(bf16[2,4096,384]{2,1,0:T(8,128)(2,1)} %bitcast.20, bf16[2,4096,1536]{2,1,0:T(8,128)(2,1)} %bitcast.18), kind=kOutput, calls=%fused_computation | convolution fusion | flops 9663676416 | bytes 36175872 | tf_op jit(solution)/shard_map/lti,ltj->lij/dot_general | solution.py:346
  227.6 20.1 %convolution_bitcast_fusion.1 = f32[1,2,1536,384]{3,2,1,0:T(8,128)} fusion(bf16[2,4096,1536]{2,1,0:T(8,128)(2,1)} %bitcast.17, bf16[2,4096,384]{2,1,0:T(8,128)(2,1)} %bitcast.19), kind=kOutput, calls=%fused_computation.1 | convolution fusion | flops 9663676416 | bytes 36175872 | tf_op jit(solution)/shard_map/lti,ltj->lij/dot_general | solution.py:346
